TPU v7x, 512 devices: a whole 4x8x8 slice. The times are simulated.
512 devices in a mesh: clip: 8 (over z_hi, x), seq: 64 (over y, z_lo, core).
Axes of the slice: x: 4, y: 8, z: 8 (z_hi: 2, z_lo: 4; z = z_hi * 4 + z_lo), core: 2. Of those that a mesh axis runs over, the one named last changes fastest.
Arguments:
- spatial_saved: bfloat16 [3, 512, 256, 576], P(None, ('clip', 'seq')), parts along dimension 1, may hold values from -48 to 48
- hidden: bfloat16 [512, 256, 1152], P(('clip', 'seq')), parts along dimension 0, may hold values from -6 to 6
- temporal_out_grad: bfloat16 [512, 256, 576], P(('clip', 'seq')), parts along dimension 0, may hold values from -6 to 6
- stream_grad: bfloat16 [512, 256, 1152], P(('clip', 'seq')), parts along dimension 0, may hold values from -6 to 6
- modulation: float32 [1152], replicated, may hold values from -0.5 to 1
- temporal_weights: bfloat16 [1152, 1728], P('seq'), may hold values from -0.1875 to 0.1875
- spatial_weights: bfloat16 [576, 1152], P('seq'), may hold values from -0.25 to 0.25
Outputs:
- hidden_grad: bfloat16 [512, 256, 1152], P(('clip', 'seq')), parts along dimension 0
- spatial_grad: bfloat16 [3, 512, 256, 576], P(None, ('clip', 'seq')), parts along dimension 1
There are 8 independent parts, one for each index of `clip`. A program takes and returns all parts, laid end to end along the dimension named above; an argument that names none is the same for every part. Nothing has to cross between parts.
All inputs are finite; a program needn't handle non-finite values.
Results may differ from a plain program's by a relative error of at most 0.024.
Values may be sent and summed in bfloat16 or wider, within the bound.
A program may use at most 64 MiB of HBM per device.

v0:
```python
import math
import jax
import jax.numpy as jnp
from jax import lax
from jax.sharding import PartitionSpec as P

HEADS = 8
HD = 72
epsilon = 1e-06


def attend_grad(query, keys, values, grad_o, form):
    key_form = form.replace("l", "m")
    scale = 1.0 / math.sqrt(query.shape[-1])
    scores = (
        jnp.einsum(
            form + "," + key_form + "->bhlm", query, keys, preferred_element_type=jnp.float32
        )
        * scale
    )
    attention = jax.nn.softmax(scores, axis=-1)
    rounded = attention.astype(jnp.bfloat16)
    output = jnp.einsum(
        "bhlm," + key_form + "->" + form, rounded, values, preferred_element_type=jnp.float32
    )
    delta = jnp.einsum(form + "," + form + "->bhl", grad_o.astype(jnp.float32), output)
    spread = jnp.einsum(
        form + "," + key_form + "->bhlm", grad_o, values, preferred_element_type=jnp.float32
    )
    dscore = (attention * (spread - delta[..., None])).astype(jnp.bfloat16)
    grad_query = jnp.einsum(
        "bhlm," + key_form + "->" + form, dscore, keys, preferred_element_type=jnp.float32
    )
    grad_keys = jnp.einsum(
        "bhlm," + form + "->" + key_form, dscore, query, preferred_element_type=jnp.float32
    )
    grad_values = jnp.einsum(
        "bhlm," + form + "->" + key_form, rounded, grad_o, preferred_element_type=jnp.float32
    )
    return (
        (grad_query * scale).astype(jnp.bfloat16),
        (grad_keys * scale).astype(jnp.bfloat16),
        grad_values.astype(jnp.bfloat16),
    )


def split_heads(block):
    return block.reshape(block.shape[:-1] + (HEADS, HD))


def merge_heads(block):
    return block.reshape(block.shape[:-2] + (HEADS * HD,))


def layer_norm(hidden, modulation):
    widened = hidden.astype(jnp.float32)
    mean_value = jnp.mean(widened, axis=-1, keepdims=True)
    centered = widened - mean_value
    inverse = lax.rsqrt(jnp.mean(centered * centered, axis=-1, keepdims=True) + epsilon)
    normal_form = centered * inverse
    normed = (normal_form * (1.0 + modulation)).astype(jnp.bfloat16)
    return (normed, normal_form, inverse)


def norm_back(grad_normed, normal_form, inverse, modulation):
    scaled = grad_normed * (1.0 + modulation)
    return inverse * (
        scaled
        - jnp.mean(scaled, axis=-1, keepdims=True)
        - normal_form * jnp.mean(scaled * normal_form, axis=-1, keepdims=True)
    )


def temporal_backward(projected, grad_patch):
    width = HEADS * HD
    grads = attend_grad(
        split_heads(projected[..., :width]),
        split_heads(projected[..., width : 2 * width]),
        split_heads(projected[..., 2 * width :]),
        split_heads(grad_patch),
        "lbhd",
    )
    return jnp.concatenate([merge_heads(gradient) for gradient in grads], axis=-1)


def shards(
    spatial_saved,
    hidden,
    temporal_out_grad,
    stream_grad,
    modulation,
    temporal_weights,
    spatial_weights,
):
    grad_patch = lax.all_to_all(temporal_out_grad, "seq", split_axis=1, concat_axis=0, tiled=True)
    normed, normal_form, inverse = layer_norm(hidden, modulation)
    projected = jnp.einsum(
        "fpd,dc->fpc",
        normed,
        lax.all_gather(temporal_weights, "seq", axis=0, tiled=True),
        preferred_element_type=jnp.float32,
    ).astype(jnp.bfloat16)
    projected_patch = lax.all_to_all(projected, "seq", split_axis=1, concat_axis=0, tiled=True)
    grads_patch = temporal_backward(projected_patch, grad_patch)
    projection_grads = lax.all_to_all(grads_patch, "seq", split_axis=0, concat_axis=1, tiled=True)
    branch = norm_back(
        jnp.einsum(
            "fpc,dc->fpd",
            projection_grads,
            lax.all_gather(temporal_weights, "seq", axis=0, tiled=True),
            preferred_element_type=jnp.float32,
        ),
        normal_form,
        inverse,
        modulation,
    ).astype(jnp.bfloat16)
    branch = lax.optimization_barrier(branch)
    hidden_grad = (stream_grad.astype(jnp.float32) + branch.astype(jnp.float32)).astype(
        jnp.bfloat16
    )
    attention_grad = jnp.einsum(
        "fpd,cd->fpc",
        hidden_grad,
        lax.all_gather(spatial_weights, "seq", axis=0, tiled=True),
        preferred_element_type=jnp.float32,
    ).astype(jnp.bfloat16)
    spatial = attend_grad(
        split_heads(spatial_saved[0]),
        split_heads(spatial_saved[1]),
        split_heads(spatial_saved[2]),
        split_heads(attention_grad),
        "blhd",
    )
    spatial_grad = jnp.stack([merge_heads(gradient) for gradient in spatial])
    return (hidden_grad, spatial_grad)


def solution(mesh):
    return jax.shard_map(
        shards,
        mesh=mesh,
        in_specs=(
            P(None, ("clip", "seq"), None, None),
            P(("clip", "seq"), None, None),
            P(("clip", "seq"), None, None),
            P(("clip", "seq"), None, None),
            P(),
            P("seq", None),
            P("seq", None),
        ),
        out_specs=(P(("clip", "seq"), None, None), P(None, ("clip", "seq"), None, None)),
        check_vma=False,
    )
```

profile of v0, /device:TPU:1, one launch (start us, length us, event | category | flops | bytes accessed | tf_op | source)
XLA Modules:
  0.0 332.2 jit_solution(14576115687310509611)
XLA Ops:
  9.9 2.7 reduce.18
  13.7 15.3 %all-to-all-start.1 = ((bf16[64,2,1152]{2,1,0:T(2,128)(2,1)}), bf16[64,2,1152]{2,1,0:T(2,128)(2,1)}, u32[]{:S(2)}, u32[]{:S(2)}) async-start(bf16[64,2,1152]{2,1,0:T(2,128)(2,1)} %reshape.205), calls=%async_computation.1 | async-start | bytes 589824 | tf_op jit(solution)/shard_map/all_to_all | solution.py:95
  29.5 108.3 %all-gather.5.cloned.1.call-done = bf16[64,18,1728]{2,1,0:T(8,128)(2,1)} async-done(((bf16[1,18,1728]{2,1,0:T(8,128)(2,1)}), bf16[64,18,1728]{2,1,0:T(8,128)(2,1)}) %all-gather.5.cloned.1.call-update) | async-done | bytes 3981328 | tf_op jit(solution)/shard_map/all_gather | solution.py:100
  137.8 7.7 %reshape.189 = bf16[1152,1728]{1,0:T(8,128)(2,1)} reshape(bf16[64,18,1728]{2,1,0:T(8,128)(2,1)} %all-gather.5.cloned.1.call-done) | data formatting | bytes 7962624
  145.5 4.0 %fusion.2 = bf16[1,256,1728]{1,2,0:T(8,128)(2,1)S(1)} fusion(bf16[1152,1728]{1,0:T(8,128)(2,1)} %reshape.189, bf16[1,256,1152]{2,1,0:T(8,128)(2,1)S(1)} %copy-done, f32[1152]{0:T(1024)S(1)} %broadcast_add_fusion, f32[256]{0:T(256)S(1)} %add_rsqrt_fusion, f32[256]{0:T(256)S(1)} %broadcast_multiply_fusion.2), kind=kOutput, calls=%fused_computation.4 | convolution fusion | flops 1021132800 | bytes 5462528 | tf_op jit(solution)/shard_map/fpd,dc->fpc/dot_general | solution.py:97
  149.5 2.8 copy.37
  152.4 6.5 %reduce.17 = bf16[256,1728]{1,0:T(8,128)(2,1)S(1)} reduce(bf16[256,1,1728]{2,1,0:T(2,128)(2,1)S(1)} %bitcast.102, bf16[]{:T(256)} %broadcast.92), dimensions={1}, to_apply=%bitcast.78.reduce_sub_computation | reduce | bytes 1769474
  158.8 1.9 reshape.203
  160.8 7.6 %all-to-all-start = ((bf16[64,2,3456]{2,1,0:T(2,128)(2,1)}), bf16[64,2,3456]{2,1,0:T(2,128)(2,1)S(1)}, u32[]{:S(2)}, u32[]{:S(2)}) async-start(bf16[64,2,3456]{2,1,0:T(2,128)(2,1)} %reshape.203), calls=%async_computation | async-start | bytes 1769472 | tf_op jit(solution)/shard_map/all_to_all | solution.py:103
  168.4 10.9 %all-gather.7.cloned.1.call-start = ((), (), s32[]{:S(2)}) async-start(), calls=%async_computation.4 | async-start | bytes 2396160 | tf_op jit(solution)/shard_map/all_gather | solution.py:124
  179.4 2.5 reshape.206
  181.9 1.8 bitcast_reduce_fusion.1
  185.1 8.2 %all-to-all-done = bf16[64,2,3456]{2,1,0:T(2,128)(2,1)S(1)} async-done(((bf16[64,2,3456]{2,1,0:T(2,128)(2,1)}), bf16[64,2,3456]{2,1,0:T(2,128)(2,1)S(1)}, u32[]{:S(2)}, u32[]{:S(2)}) %all-to-all-start) | async-done | bytes 884768 | tf_op jit(solution)/shard_map/all_to_all | solution.py:103
  194.8 5.1 %bitcast_reduce_fusion = bf16[256,1728]{1,0:T(8,128)(2,1)S(1)} fusion(bf16[256,1,1728]{2,1,0:T(2,128)(2,1)S(1)} %reshape.204), kind=kLoop, calls=%fused_computation.80 | loop fusion | bytes 1769472 | tf_op jit(solution)/shard_map/all_to_all | solution.py:103
  204.0 1.7 convolution_bitcast_fusion
  206.6 1.7 fusion.13
  210.5 1.7 fusion.18
  213.4 1.7 copy.55
  215.1 6.2 %all-to-all-start.2 = ((bf16[64,4,1728]{2,1,0:T(4,128)(2,1)}), bf16[64,4,1728]{2,1,0:T(4,128)(2,1)S(1)}, u32[]{:S(2)}, u32[]{:S(2)}) async-start(bf16[64,4,1728]{2,1,0:T(4,128)(2,1)} %copy.55), calls=%async_computation.2 | async-start | bytes 1835008 | tf_op jit(solution)/shard_map/all_to_all | solution.py:105
  222.0 2.2 fusion.67
  224.2 1.8 fusion.29
  226.0 83.0 %all-gather.7.cloned.1.call-done = bf16[64,9,1152]{2,1,0:T(8,128)(2,1)} async-done(((bf16[1,9,1152]{2,1,0:T(8,128)(2,1)}), bf16[64,9,1152]{2,1,0:T(8,128)(2,1)}) %all-gather.7.cloned.1.call-update) | async-done | bytes 1327120 | tf_op jit(solution)/shard_map/all_gather | solution.py:124
  309.0 3.7 %reshape.191 = bf16[576,1152]{1,0:T(8,128)(2,1)} reshape(bf16[64,9,1152]{2,1,0:T(8,128)(2,1)} %all-gather.7.cloned.1.call-done) | data formatting | bytes 2654208
  314.1 3.9 %fusion.23 = (f32[256]{0:T(256)S(1)}, f32[256,1152]{1,0:T(8,128)S(1)}) fusion(bf16[1,256,1152]{2,1,0:T(8,128)(2,1)S(1)} %copy-done, f32[256]{0:T(256)S(1)} %add_rsqrt_fusion, f32[256]{0:T(256)S(1)} %broadcast_multiply_fusion.2, f32[1152]{0:T(1024)S(1)} %broadcast_add_fusion, bf16[256,1728]{1,0:T(8,128)(2,1)} %reshape.181, bf16[1152,1728]{1,0:T(8,128)(2,1)} %reshape.189), kind=kOutput, calls=%fused_computation.41 | convolution fusion | flops 1020985088 | bytes 6643200 | tf_op jit(solution)/shard_map/fpc,dc->fpd/dot_general | solution.py:107
  (63 shorter events, 24.4 us)
Async XLA Ops:
  7.2 130.7 %all-gather.5.cloned.1.call-start = ((), (), s32[]{:S(2)}) async-start(), calls=%async_computation.3 | async-start | bytes 5591040 | tf_op jit(solution)/shard_map/all_gather | solution.py:100
  9.3 19.7 %copy-start = (bf16[1,256,1152]{2,1,0:T(8,128)(2,1)S(1)}, bf16[1,256,1152]{2,1,0:T(8,128)(2,1)}, u32[]{:S(2)}) copy-start(bf16[1,256,1152]{2,1,0:T(8,128)(2,1)} %param.8) | copy-start | bytes 1769476
  12.6 16.9 %copy-start.8 = (f32[1152]{0:T(1024)S(1)}, f32[1152]{0:T(1024)}, u32[]{:S(2)}) copy-start(f32[1152]{0:T(1024)} %param.11) | copy-start | bytes 13828
  13.7 147.1 %all-to-all-start.1 = ((bf16[64,2,1152]{2,1,0:T(2,128)(2,1)}), bf16[64,2,1152]{2,1,0:T(2,128)(2,1)}, u32[]{:S(2)}, u32[]{:S(2)}) async-start(bf16[64,2,1152]{2,1,0:T(2,128)(2,1)} %reshape.205), calls=%async_computation.1 | async-start | bytes 589824 | tf_op jit(solution)/shard_map/all_to_all | solution.py:95
  160.8 32.6 %all-to-all-start = ((bf16[64,2,3456]{2,1,0:T(2,128)(2,1)}), bf16[64,2,3456]{2,1,0:T(2,128)(2,1)S(1)}, u32[]{:S(2)}, u32[]{:S(2)}) async-start(bf16[64,2,3456]{2,1,0:T(2,128)(2,1)} %reshape.203), calls=%async_computation | async-start | bytes 1769472 | tf_op jit(solution)/shard_map/all_to_all | solution.py:103
  168.4 140.6 %all-gather.7.cloned.1.call-start = ((), (), s32[]{:S(2)}) async-start(), calls=%async_computation.4 | async-start | bytes 2396160 | tf_op jit(solution)/shard_map/all_gather | solution.py:124
  204.0 1.7 copy-start.2
  215.1 6.2 %copy-start.5 = (bf16[3,1,256,576]{2,3,1,0:T(8,128)(2,1)S(1)}, bf16[3,1,256,576]{2,3,1,0:T(8,128)(2,1)}, u32[]{:S(2)}) copy-start(bf16[3,1,256,576]{2,3,1,0:T(8,128)(2,1)} %param.7) | copy-start | bytes 2654212
  215.1 97.7 %all-to-all-start.2 = ((bf16[64,4,1728]{2,1,0:T(4,128)(2,1)}), bf16[64,4,1728]{2,1,0:T(4,128)(2,1)S(1)}, u32[]{:S(2)}, u32[]{:S(2)}) async-start(bf16[64,4,1728]{2,1,0:T(4,128)(2,1)} %copy.55), calls=%async_computation.2 | async-start | bytes 1835008 | tf_op jit(solution)/shard_map/all_to_all | solution.py:105
  318.2 1.1 copy-start.6
  319.2 1.3 copy-start.3
  319.2 1.9 copy-start.4
  320.6 0.9 copy-start.7
  320.6 1.8 copy-start.1
Sparse Core Ops, SparseCore 0:
  10.1 127.6 all-gather.4
  179.5 129.4 all-gather.6
where the time goes:
time: 336 us; the launch traced here: 332 us
  waiting for transfers between devices  200 us (60%)
  local copies, waits for them, and re-layouts  43.1 us (13%)
  starting transfers between devices  40.1 us (12%)
  matrix products  20.2 us (6%)
  between operations  14.6 us (4%)
  other arithmetic  13.9 us (4%)
    all_gather x1, waiting for transfers between devices, shards(): lax.all_gather(temporal_weights, 'seq', axis=0, tiled=True)  108 us
    all_gather x1, waiting for transfers between devices, shards(): lax.all_gather(spatial_weights, 'seq', axis=0, tiled=True)  83 us
    unnamed x26, local copies, waits for them, and re-layouts  23.1 us
    all_to_all x1, starting transfers between devices, shards(): lax.all_to_all(temporal_out_grad, 'seq', split_axis=1, concat_axis=0, til...  15.3 us
    all_gather x1, starting transfers between devices, shards(): lax.all_gather(spatial_weights, 'seq', axis=0, tiled=True)  10.9 us
    unnamed x3, other arithmetic  9.99 us
    all_to_all x1, waiting for transfers between devices, shards(): lax.all_to_all(projected, 'seq', split_axis=1, concat_axis=0, tiled=True)  8.25 us
    all_to_all x1, starting transfers between devices, shards(): lax.all_to_all(projected, 'seq', split_axis=1, concat_axis=0, tiled=True)  7.62 us
  transfers between devices with their start and end apart: 5, of which 3 were waited for; matrix products, arithmetic and copies ran while one was open for 19% of the time, Pallas kernels for 0%

commit v1 on v0

--- a/solution.py
+++ b/solution.py
@@ -7,6 +7,11 @@
 HEADS = 8
 HD = 72
 epsilon = 1e-06
+
+
+def swapped_in(x, axis, along):
+    sent = jnp.stack([x] * lax.axis_size(axis))
+    return jnp.concatenate(lax.all_to_all(sent, axis, 0, 0), axis=along)
 
 
 def attend_grad(query, keys, values, grad_o, form):
@@ -97,7 +102,7 @@
     projected = jnp.einsum(
         "fpd,dc->fpc",
         normed,
-        lax.all_gather(temporal_weights, "seq", axis=0, tiled=True),
+        swapped_in(temporal_weights, "seq", 0),
         preferred_element_type=jnp.float32,
     ).astype(jnp.bfloat16)
     projected_patch = lax.all_to_all(projected, "seq", split_axis=1, concat_axis=0, tiled=True)

time: 336 us -> 410 us (1.22)
  waiting for transfers between devices: 200 us -> 251 us
  local copies, waits for them, and re-layouts: 43.1 us -> 53.8 us
  starting transfers between devices: 40.1 us -> 50.3 us
    all_to_all x0 -> x1, waiting for transfers between devices: none -> 123 us  [swapped_in(): return jnp.concatenate(lax.all_to_all(sent, axis, 0, 0), axis=along)]
    all_gather x1, waiting for transfers between devices: 83 us -> 0.02 us  [shards(): lax.all_gather(spatial_weights, 'seq', axis=0, tiled=True)]
    all_to_all x0 -> x1, starting transfers between devices: none -> 14.9 us  [swapped_in(): return jnp.concatenate(lax.all_to_all(sent, axis, 0, 0), axis=along)]
    all_to_all x1, waiting for transfers between devices: 8.25 us -> 20.8 us  [shards(): lax.all_to_all(projected, 'seq', split_axis=1, concat_axis=0, tiled=True)]
    all_gather x1, starting transfers between devices: 10.9 us -> 0.04 us  [shards(): lax.all_gather(spatial_weights, 'seq', axis=0, tiled=True)]
    reshape x0 -> x1, local copies, waits for them, and re-layouts: none -> 7.75 us  [swapped_in(): return jnp.concatenate(lax.all_to_all(sent, axis, 0, 0), axis=along)]
    unnamed x26 -> x28, local copies, waits for them, and re-layouts: 23.1 us -> 22.5 us
  transfers between devices with their start and end apart: 5 -> 6, of which waited for: 3 -> 3; matrix products, arithmetic and copies ran while one was open for 19% -> 18% of each run, Pallas kernels for 0% -> 0%
where the time goes in v1:
time: 410 us; the launch traced here: 404 us
  waiting for transfers between devices  251 us (61%)
  local copies, waits for them, and re-layouts  53.8 us (13%)
  starting transfers between devices  50.3 us (12%)
  matrix products  20.2 us (5%)
  between operations  14.6 us (4%)
  other arithmetic  13.9 us (3%)
    all_to_all x1, waiting for transfers between devices, swapped_in(): return jnp.concatenate(lax.all_to_all(sent, axis, 0, 0), axis=along)  123 us
    all_gather x1, waiting for transfers between devices, shards(): lax.all_gather(temporal_weights, 'seq', axis=0, tiled=True)  106 us
    unnamed x28, local copies, waits for them, and re-layouts  22.5 us
    all_to_all x1, waiting for transfers between devices, shards(): lax.all_to_all(projected, 'seq', split_axis=1, concat_axis=0, tiled=True)  20.8 us
    all_to_all x1, starting transfers between devices, shards(): lax.all_to_all(temporal_out_grad, 'seq', split_axis=1, concat_axis=0, til...  18.8 us
    all_to_all x1, starting transfers between devices, swapped_in(): return jnp.concatenate(lax.all_to_all(sent, axis, 0, 0), axis=along)  14.9 us
    all_to_all x1, starting transfers between devices, shards(): lax.all_to_all(projected, 'seq', split_axis=1, concat_axis=0, tiled=True)  10.6 us
    unnamed x3, other arithmetic  10 us
  transfers between devices with their start and end apart: 6, of which 3 were waited for; matrix products, arithmetic and copies ran while one was open for 18% of the time, Pallas kernels for 0%

profile of v1, /device:TPU:1, one launch (start us, length us, event | category | flops | bytes accessed | tf_op | source)
XLA Modules:
  0.0 404.3 jit_solution(5011394023485326789)
XLA Ops:
  7.2 3.6 stack.4
  10.8 14.9 %all-to-all-start = ((bf16[64,18,1728]{2,1,0:T(8,128)(2,1)}), bf16[64,18,1728]{2,1,0:T(8,128)(2,1)}, u32[]{:S(2)}, u32[]{:S(2)}) async-start(bf16[64,18,1728]{2,1,0:T(8,128)(2,1)} %stack.4), calls=%async_computation | async-start | bytes 11010048 | tf_op jit(solution)/shard_map/all_to_all | solution.py:14
  28.3 2.7 reduce.18
  32.6 122.7 %all-to-all-done = bf16[64,18,1728]{2,1,0:T(8,128)(2,1)} async-done(((bf16[64,18,1728]{2,1,0:T(8,128)(2,1)}), bf16[64,18,1728]{2,1,0:T(8,128)(2,1)}, u32[]{:S(2)}, u32[]{:S(2)}) %all-to-all-start) | async-done | bytes 3981344 | tf_op jit(solution)/shard_map/all_to_all | solution.py:14
  155.3 18.8 %all-to-all-start.2 = ((bf16[64,2,1152]{2,1,0:T(2,128)(2,1)}), bf16[64,2,1152]{2,1,0:T(2,128)(2,1)}, u32[]{:S(2)}, u32[]{:S(2)}) async-start(bf16[64,2,1152]{2,1,0:T(2,128)(2,1)} %reshape.211), calls=%async_computation.2 | async-start | bytes 589824 | tf_op jit(solution)/shard_map/all_to_all | solution.py:100
  174.1 7.8 %reshape.179 = bf16[1152,1728]{1,0:T(8,128)(2,1)} reshape(bf16[64,18,1728]{2,1,0:T(8,128)(2,1)} %all-to-all-done) | data formatting | bytes 7962624 | tf_op jit(solution)/shard_map/reshape | solution.py:14
  181.8 4.0 fusion.2
  185.9 2.8 copy.37
  188.7 6.5 %reduce.17 = bf16[256,1728]{1,0:T(8,128)(2,1)S(1)} reduce(bf16[256,1,1728]{2,1,0:T(2,128)(2,1)S(1)} %bitcast.102, bf16[]{:T(256)} %broadcast.94), dimensions={1}, to_apply=%bitcast.78.reduce_sub_computation | reduce | bytes 1769474
  195.1 1.9 reshape.209
  197.1 10.6 %all-to-all-start.1 = ((bf16[64,2,3456]{2,1,0:T(2,128)(2,1)}), bf16[64,2,3456]{2,1,0:T(2,128)(2,1)S(1)}, u32[]{:S(2)}, u32[]{:S(2)}) async-start(bf16[64,2,3456]{2,1,0:T(2,128)(2,1)} %reshape.209), calls=%async_computation.1 | async-start | bytes 1769472 | tf_op jit(solution)/shard_map/all_to_all | solution.py:108
  207.7 2.5 reshape.212
  210.2 1.8 bitcast_reduce_fusion.1
  213.4 20.8 %all-to-all-done.1 = bf16[64,2,3456]{2,1,0:T(2,128)(2,1)S(1)} async-done(((bf16[64,2,3456]{2,1,0:T(2,128)(2,1)}), bf16[64,2,3456]{2,1,0:T(2,128)(2,1)S(1)}, u32[]{:S(2)}, u32[]{:S(2)}) %all-to-all-start.1) | async-done | bytes 884768 | tf_op jit(solution)/shard_map/all_to_all | solution.py:108
  235.9 5.1 %bitcast_reduce_fusion = bf16[256,1728]{1,0:T(8,128)(2,1)S(1)} fusion(bf16[256,1,1728]{2,1,0:T(2,128)(2,1)S(1)} %reshape.210), kind=kLoop, calls=%fused_computation.80 | loop fusion | bytes 1769472 | tf_op jit(solution)/shard_map/all_to_all | solution.py:108
  247.6 1.7 fusion.13
  251.5 1.7 fusion.18
  256.2 6.0 %all-to-all-start.3 = ((bf16[64,4,1728]{2,1,0:T(4,128)(2,1)}), bf16[64,4,1728]{2,1,0:T(4,128)(2,1)S(1)}, u32[]{:S(2)}, u32[]{:S(2)}) async-start(bf16[64,4,1728]{2,1,0:T(4,128)(2,1)} %copy.55), calls=%async_computation.3 | async-start | bytes 1835008 | tf_op jit(solution)/shard_map/all_to_all | solution.py:110
  263.0 2.1 fusion.67
  265.1 1.8 fusion.29
  266.9 3.7 reshape.197
  270.7 106.4 %all-gather.5.cloned.1.call-done = bf16[64,18,1728]{2,1,0:T(8,128)(2,1)} async-done(((bf16[1,18,1728]{2,1,0:T(8,128)(2,1)}), bf16[64,18,1728]{2,1,0:T(8,128)(2,1)}) %all-gather.5.cloned.1.call-update) | async-done | bytes 3981328 | tf_op jit(solution)/shard_map/all_gather | solution.py:115
  377.1 7.7 %reshape.195 = bf16[1152,1728]{1,0:T(8,128)(2,1)} reshape(bf16[64,18,1728]{2,1,0:T(8,128)(2,1)} %all-gather.5.cloned.1.call-done) | data formatting | bytes 7962624
  386.2 3.9 fusion.23
  (69 shorter events, 27.9 us)
Async XLA Ops:
  10.8 16.4 %copy-start.8 = (bf16[1,256,576]{1,2,0:T(8,128)(2,1)S(1)}, bf16[1,256,576]{1,2,0:T(8,128)(2,1)}, u32[]{:S(2)}) copy-start(bf16[1,256,576]{1,2,0:T(8,128)(2,1)} %param.9) | copy-start | bytes 884740
  10.8 144.5 %all-to-all-start = ((bf16[64,18,1728]{2,1,0:T(8,128)(2,1)}), bf16[64,18,1728]{2,1,0:T(8,128)(2,1)}, u32[]{:S(2)}, u32[]{:S(2)}) async-start(bf16[64,18,1728]{2,1,0:T(8,128)(2,1)} %stack.4), calls=%async_computation | async-start | bytes 11010048 | tf_op jit(solution)/shard_map/all_to_all | solution.py:14
  25.6 241.3 %all-gather.7.cloned.1.call-start = ((), (), s32[]{:S(2)}) async-start(), calls=%async_computation.5 | async-start | bytes 2396160 | tf_op jit(solution)/shard_map/all_gather | solution.py:129
  26.4 5.7 %copy-start = (bf16[1,256,1152]{2,1,0:T(8,128)(2,1)S(1)}, bf16[1,256,1152]{2,1,0:T(8,128)(2,1)}, u32[]{:S(2)}) copy-start(bf16[1,256,1152]{2,1,0:T(8,128)(2,1)} %param.8) | copy-start | bytes 1769476
  26.4 350.7 %all-gather.5.cloned.1.call-start = ((), (), s32[]{:S(2)}) async-start(), calls=%async_computation.4 | async-start | bytes 5591040 | tf_op jit(solution)/shard_map/all_gather | solution.py:115
  28.3 4.3 %copy-start.9 = (f32[1152]{0:T(1024)S(1)}, f32[1152]{0:T(1024)}, u32[]{:S(2)}) copy-start(f32[1152]{0:T(1024)} %param.11) | copy-start | bytes 13828
  155.3 41.8 %all-to-all-start.2 = ((bf16[64,2,1152]{2,1,0:T(2,128)(2,1)}), bf16[64,2,1152]{2,1,0:T(2,128)(2,1)}, u32[]{:S(2)}, u32[]{:S(2)}) async-start(bf16[64,2,1152]{2,1,0:T(2,128)(2,1)} %reshape.211), calls=%async_computation.2 | async-start | bytes 589824 | tf_op jit(solution)/shard_map/all_to_all | solution.py:100
  197.1 37.1 %all-to-all-start.1 = ((bf16[64,2,3456]{2,1,0:T(2,128)(2,1)}), bf16[64,2,3456]{2,1,0:T(2,128)(2,1)S(1)}, u32[]{:S(2)}, u32[]{:S(2)}) async-start(bf16[64,2,3456]{2,1,0:T(2,128)(2,1)} %reshape.209), calls=%async_computation.1 | async-start | bytes 1769472 | tf_op jit(solution)/shard_map/all_to_all | solution.py:108
  245.0 1.7 copy-start.2
  256.2 6.0 %copy-start.5 = (bf16[3,1,256,576]{2,3,1,0:T(8,128)(2,1)S(1)}, bf16[3,1,256,576]{2,3,1,0:T(8,128)(2,1)}, u32[]{:S(2)}) copy-start(bf16[3,1,256,576]{2,3,1,0:T(8,128)(2,1)} %param.7) | copy-start | bytes 2654212
  256.2 128.7 %all-to-all-start.3 = ((bf16[64,4,1728]{2,1,0:T(4,128)(2,1)}), bf16[64,4,1728]{2,1,0:T(4,128)(2,1)S(1)}, u32[]{:S(2)}, u32[]{:S(2)}) async-start(bf16[64,4,1728]{2,1,0:T(4,128)(2,1)} %copy.55), calls=%async_computation.3 | async-start | bytes 1835008 | tf_op jit(solution)/shard_map/all_to_all | solution.py:110
  390.3 1.1 copy-start.6
  391.3 1.3 copy-start.3
  391.3 1.9 copy-start.4
  392.7 0.9 copy-start.7
  392.7 1.8 copy-start.1
Sparse Core Ops, SparseCore 0:
  28.6 211.5 all-gather.6
  242.4 134.6 all-gather.4
